TPU v7x, 256 devices: a whole 4x4x8 slice. The times are simulated.
256 devices in a mesh: dp: 8 (over y, core), tensor: 32 (over z, x).
Axes of the slice: x: 4, y: 4, z: 8, core: 2. Of those that a mesh axis runs over, the one named last changes fastest.
Arguments:
- hidden: bfloat16 [1280, 16384], P(None, ('dp', 'tensor')), may hold values from -100 to 100
- gain: bfloat16 [1, 16384], P(None, ('dp', 'tensor')), may hold values from 0.5 to 2, as said below
- head_weight: bfloat16 [16384, 65536], P('dp', 'tensor'), may hold values from -3 to 3
- draft_probs: float32 [1280, 65536], P(('dp', 'tensor')), may hold values from 0 to 1, as said below
- draft_ids: int32 [1280], P('dp'), may hold values from 0 to 65535
- reject_at: int32 [256], P('dp'), may hold values from 0 to 4
Outputs:
- token_logprob: float32 [1280], P('dp')
- residual: float32 [256, 65536], P('dp', 'tensor')
Inputs may be any that keep to these rules, and one draw needn't show every extreme that they name: `draft_probs`: every row is a probability distribution over the 65536 entries that sums to one. `gain`: positive.
All inputs are finite; a program needn't handle non-finite values.
Results may differ from a plain program's by a relative error of at most 0.0005.
The roundings to bfloat16 on the way count: a program that leaves them out, or rounds other values in their place, can miss the bound.
Values may be sent and summed in bfloat16 or wider, within the bound.
A program may use at most 128 MiB of HBM per device.

v0:
```python
import jax
import jax.numpy as jnp
from jax import lax
from jax.sharding import Mesh
from jax.sharding import PartitionSpec as P

D = 16384
VOCAB = 65536
POS = 5
TENSOR = ("tensor_0", "tensor_1")
DP_TENSOR = ("dp", "tensor_0", "tensor_1")


EPS = 1e-05


def gather_turned(arrays, axis, dims):
    turned = [jnp.moveaxis(a, dim, 0) for a, dim in zip(arrays, dims)]
    widths = [t[0].size for t in turned]
    both = jnp.concatenate([t.reshape(-1, w) for t, w in zip(turned, widths)], axis=1)
    out = lax.all_gather(both, axis, axis=0, tiled=True)
    tiles = jnp.split(out, [sum(widths[:k]) for k in range(1, len(widths))], axis=1)
    return tuple(
        (
            jnp.moveaxis(b.reshape(-1, *t.shape[1:]), 0, dim)
            for b, t, dim in zip(tiles, turned, dims)
        )
    )


def sent_to_all(shard, axis):
    devices = lax.axis_size(axis)
    return lax.all_to_all(
        jnp.broadcast_to(shard[None], (devices, *shard.shape)), axis, 0, 0, tiled=True
    )


def of_everyone(shard, axis):
    everything = sent_to_all(shard, axis)
    return jnp.sum(everything, axis=0)


def collected_together(shard, axis):
    leaves = jax.tree.leaves(shard)
    order = sorted(range(len(leaves)), key=lambda k: -leaves[k].size)
    width = (1, *leaves[order[0]].shape)[-1]
    lines = [
        jnp.pad(leaves[k].reshape(-1), (0, -leaves[k].size % width)).reshape(-1, width)
        for k in order
    ]
    both, at, found = (sent_to_all(jnp.concatenate(lines), axis), 0, {})
    for k, line in zip(order, lines):
        share = both[:, at : at + len(line)].reshape(len(both), -1)
        found[k] = share[:, : leaves[k].size].reshape(-1, *leaves[k].shape)
        at += len(line)
    numbers = iter(range(len(leaves)))
    return jax.tree.map(lambda _: found[next(numbers)], shard)


def combined_pairwise(pieces, combine):
    while len(jax.tree.leaves(pieces)[0]) > 1:
        pieces = jax.vmap(combine)(
            *(jax.tree.map(lambda part: part[side::2], pieces) for side in (0, 1))
        )
    return jax.tree.map(lambda part: part[0], pieces)


def merged(shard, axis, combine):
    pieces = collected_together(shard, axis)
    return combined_pairwise(pieces, combine)


def in_blocks(shard, dim, devices):
    before, after = (shard.shape[:dim], shard.shape[dim + 1 :])
    return jnp.moveaxis(shard.reshape(*before, devices, -1, *after), dim, 0)


def laid_out(tiles, dim):
    tiles = jnp.moveaxis(tiles, 0, dim)
    shape = tiles.shape
    return tiles.reshape(*shape[:dim], shape[dim] * shape[dim + 1], *shape[dim + 2 :])


def exchange_in_order(tiles, axes, order):
    inside = tiles.shape[1:]
    out = tiles.reshape(*(lax.axis_size(a) for a in axes), *inside)
    for k in order:
        out = lax.all_to_all(out, axes[k], k, k, tiled=True)
    return out.reshape(-1, *inside)


def stepwise_exchange(shard, axes, order, split_dim, concat_dim):
    tiles = in_blocks(shard, split_dim, lax.axis_size(axes))
    return laid_out(exchange_in_order(tiles, axes, order), concat_dim)


def combine_stats(first, second):
    top = jnp.maximum(first[0], second[0])
    total = first[1] * jnp.exp(first[0] - top) + second[1] * jnp.exp(second[0] - top)
    return (top, total, first[2] + second[2])


def shards(hidden, gain, head_weight, draft_probs, draft_ids, reject_at):
    raw, gains = gather_turned((hidden, gain), TENSOR, (1, 1))
    values = raw.astype(jnp.float32)
    squares = of_everyone(jnp.sum(values * values, axis=1), "dp")
    normed = (values * lax.rsqrt(squares / D + EPS)[:, None] * gains.astype(jnp.float32)).astype(
        jnp.bfloat16
    )
    logits = lax.psum_scatter(
        jnp.dot(normed, head_weight, preferred_element_type=jnp.float32),
        "dp",
        scatter_dimension=0,
        tiled=True,
    )
    width = logits.shape[1]
    columns = lax.broadcasted_iota(jnp.int32, (1, width), 1) + lax.axis_index(TENSOR) * width
    local_max = jnp.max(logits, axis=1)
    local_pick = jnp.sum(jnp.where(columns == draft_ids[:, None], logits, 0.0), axis=1)
    local_total = jnp.sum(jnp.exp(logits - local_max[:, None]), axis=1)
    top, total, picked = merged((local_max, local_total, local_pick), TENSOR, combine_stats)
    logz = top + jnp.log(total)
    token_logprob = picked - logz
    requests = reject_at.shape[0]
    where_at = reject_at[:, None, None]
    chosen = jnp.take_along_axis(logits.reshape(requests, POS, width), where_at, axis=1)[:, 0]
    chosen_logz = jnp.take_along_axis(logz.reshape(requests, POS), reject_at[:, None], axis=1)[:, 0]
    owned = draft_probs.shape[0] // POS
    mine = lax.dynamic_slice_in_dim(reject_at, lax.axis_index(TENSOR) * owned, owned, 0)
    local_rows = jnp.take_along_axis(
        draft_probs.reshape(owned, POS, draft_probs.shape[1]), mine[:, None, None], axis=1
    )[:, 0]
    drafts = stepwise_exchange(local_rows, TENSOR, (0, 1), 1, 0)
    target = jnp.exp(chosen - chosen_logz[:, None])
    kept = jnp.maximum(target - drafts, 0.0)
    mass = of_everyone(jnp.sum(kept, axis=1), TENSOR)
    residual = VOCAB * kept / mass[:, None]
    return (token_logprob, residual)


def solution(mesh):
    finer = Mesh(mesh.devices.reshape(mesh.shape["dp"], 8, 4), ("dp", "tensor_0", "tensor_1"))
    return jax.shard_map(
        shards,
        mesh=finer,
        in_specs=(
            P(None, DP_TENSOR),
            P(None, DP_TENSOR),
            P("dp", TENSOR),
            P(DP_TENSOR, None),
            P("dp"),
            P("dp"),
        ),
        out_specs=(P("dp"), P("dp", TENSOR)),
        check_vma=False,
    )
```

profile of v0, /device:TPU:2, one launch (start us, length us, event | category | flops | bytes accessed | tf_op | source)
XLA Modules:
  0.0 244.7 jit_solution(11810999547633045622)
XLA Ops:
  7.2 0.0 all-gather.2.cloned.1.call-start
  7.2 0.8 copy.43
  8.0 1.6 pad_maximum_fusion
  9.6 0.0 all-gather.2.cloned.1.call-update
  9.6 89.8 %all-gather.2.cloned.1.call-done = bf16[2048,1281]{1,0:T(8,128)(2,1)} async-done(((bf16[64,1281]{1,0:T(8,128)(2,1)}), bf16[2048,1281]{1,0:T(8,128)(2,1)}) %all-gather.2.cloned.1.call-update) | async-done | bytes 5246992 | tf_op jit(solution)/shard_map/all_gather | solution.py:21
  99.4 3.6 %fusion = f32[1280]{0:T(1024)S(1)} fusion(bf16[2048,1281]{1,0:T(8,128)(2,1)} %all-gather.2.cloned.1.call-done), kind=kLoop, calls=%fused_computation.4 | loop fusion | flops 7863040 | bytes 5248000 | tf_op jit(solution)/shard_map/reduce_sum | solution.py:106
  103.0 0.6 broadcast_in_dim.59
  103.6 4.3 %all-to-all-start = ((f32[8,1,1280]{2,1,0:T(1,128)}), f32[8,1,1280]{2,1,0:T(1,128)S(1)}, u32[]{:S(2)}, u32[]{:S(2)}) async-start(f32[8,1,1280]{2,1,0:T(1,128)} %broadcast_in_dim.59), calls=%async_computation | async-start | bytes 81920 | tf_op jit(solution)/shard_map/all_to_all | solution.py:33
  107.9 0.0 reduce-scatter.2.cloned.1.call-start
  108.0 1.3 convert_reduce_fusion
  109.2 4.2 %all-to-all-done = f32[8,1,1280]{2,1,0:T(1,128)S(1)} async-done(((f32[8,1,1280]{2,1,0:T(1,128)}), f32[8,1,1280]{2,1,0:T(1,128)S(1)}, u32[]{:S(2)}, u32[]{:S(2)}) %all-to-all-start) | async-done | bytes 40992 | tf_op jit(solution)/shard_map/all_to_all | solution.py:33
  113.5 17.9 %fusion.3 = f32[1280,2048]{1,0:T(8,128)} fusion(bf16[2048,2048]{1,0:T(8,128)(2,1)} %param.8, f32[2048]{0:T(1024)S(1)} %convert_reduce_fusion, f32[1280]{0:T(1024)S(1)} %add_rsqrt_fusion, bf16[2048,1281]{1,0:T(8,128)(2,1)} %all-gather.2.cloned.1.call-done), kind=kOutput, calls=%fused_computation.7 | convolution fusion | flops 10747904000 | bytes 24130560 | tf_op jit(solution)/shard_map/dot_general | solution.py:111
  131.3 0.0 copy-start.2
  131.3 0.0 copy-start.1
  131.3 0.0 reduce-scatter.2.cloned.1.call-update
  131.4 0.6 copy-done.2
  132.0 0.6 dynamic_slice.3
  134.5 2.4 fusion.8
  136.9 0.8 select_n.68
  137.7 4.0 %all-to-all-start.2 = ((f32[8,4,1,2048]{3,1,2,0:T(4,128)}), f32[8,4,1,2048]{3,1,2,0:T(4,128)S(1)}, u32[]{:S(2)}, u32[]{:S(2)}) async-start(f32[8,4,1,2048]{3,1,2,0:T(4,128)} %select_n.68), calls=%async_computation.3 | async-start | bytes 524288 | tf_op jit(solution)/shard_map/all_to_all | solution.py:88
  141.8 11.8 %all-to-all-done.2 = f32[8,4,1,2048]{3,1,2,0:T(4,128)S(1)} async-done(((f32[8,4,1,2048]{3,1,2,0:T(4,128)}), f32[8,4,1,2048]{3,1,2,0:T(4,128)S(1)}, u32[]{:S(2)}, u32[]{:S(2)}) %all-to-all-start.2) | async-done | bytes 262176 | tf_op jit(solution)/shard_map/all_to_all | solution.py:88
  153.5 0.9 copy.48
  154.4 5.2 %all-to-all-start.3 = ((f32[8,4,1,2048]{3,0,2,1:T(8,128)}), f32[8,4,1,2048]{3,0,2,1:T(8,128)S(1)}, u32[]{:S(2)}, u32[]{:S(2)}) async-start(f32[8,4,1,2048]{3,0,2,1:T(8,128)} %copy.48), calls=%async_computation.4 | async-start | bytes 524288 | tf_op jit(solution)/shard_map/all_to_all | solution.py:88
  159.6 33.1 %reduce-scatter.2.cloned.1.call-done = f32[160,2048]{1,0:T(8,128)} async-done(((f32[1280,2048]{1,0:T(8,128)}), f32[160,2048]{1,0:T(8,128)}) %reduce-scatter.2.cloned.1.call-update) | async-done | bytes 1310736 | tf_op jit(solution)/shard_map/reduce_scatter | solution.py:110
  192.7 1.5 reduce_max.9
  194.1 0.0 copy-done.1
  194.1 1.8 exponential_reduce_fusion
  196.0 0.8 reshape.248
  196.8 0.0 all-to-all-done.3
  196.8 0.0 copy-start
  196.8 10.2 %all-to-all-start.1 = ((f32[32,1,480]{2,1,0:T(1,128)}), f32[32,1,480]{2,1,0:T(1,128)S(1)}, u32[]{:S(2)}, u32[]{:S(2)}) async-start(f32[32,1,480]{2,1,0:T(1,128)} %reshape.248), calls=%async_computation.2 | async-start | bytes 131072 | tf_op jit(solution)/shard_map/all_to_all | solution.py:33
  207.0 0.2 copy.49
  207.1 0.0 copy-done
  207.2 0.8 reshape_reshape.3
  208.0 1.5 reshape.176
  209.4 0.8 copy.47
  210.2 0.9 gather_fusion
  211.1 0.1 gather.23
  211.1 4.5 %all-to-all-done.1 = f32[32,1,480]{2,1,0:T(1,128)S(1)} async-done(((f32[32,1,480]{2,1,0:T(1,128)}), f32[32,1,480]{2,1,0:T(1,128)S(1)}, u32[]{:S(2)}, u32[]{:S(2)}) %all-to-all-start.1) | async-done | bytes 61472 | tf_op jit(solution)/shard_map/all_to_all | solution.py:33
  215.6 0.5 broadcast.165
  216.2 0.8 reduce.15
  217.0 0.1 reshape.249
  217.1 0.1 fusion.19
  217.8 0.5 broadcast.164
  218.3 0.7 fusion.18
  219.0 0.1 add.104
  219.1 0.7 gather_fusion.1
  219.8 0.1 sub.88
  219.9 0.1 copy.52
  220.0 0.1 broadcast_in_dim.68
  220.1 0.1 copy.50
  220.2 1.2 fusion.13
  221.4 0.1 copy.53
  221.5 0.1 broadcast_in_dim.71
  221.6 0.6 broadcast_in_dim.72
  222.2 5.3 %all-to-all-start.4 = ((f32[32,1,32]{2,1,0:T(1,128)}), f32[32,1,32]{2,1,0:T(1,128)S(1)}, u32[]{:S(2)}, u32[]{:S(2)}) async-start(f32[32,1,32]{2,1,0:T(1,128)} %broadcast_in_dim.72), calls=%async_computation.5 | async-start | bytes 32768 | tf_op jit(solution)/shard_map/all_to_all | solution.py:33
  227.5 0.6 fusion.15
  228.1 8.0 %all-to-all-done.4 = f32[32,1,32]{2,1,0:T(1,128)S(1)} async-done(((f32[32,1,32]{2,1,0:T(1,128)}), f32[32,1,32]{2,1,0:T(1,128)S(1)}, u32[]{:S(2)}, u32[]{:S(2)}) %all-to-all-start.4) | async-done | bytes 4128 | tf_op jit(solution)/shard_map/all_to_all | solution.py:33
  236.1 1.8 multiply_divide_fusion
  (45 shorter events, 0.7 us)
Async XLA Ops:
  7.2 92.2 %all-gather.2.cloned.1.call-start = ((), (), s32[]{:S(2)}) async-start(), calls=%async_computation.6 | async-start | bytes 5947392 | tf_op jit(solution)/shard_map/all_gather | solution.py:21
  103.6 9.8 %all-to-all-start = ((f32[8,1,1280]{2,1,0:T(1,128)}), f32[8,1,1280]{2,1,0:T(1,128)S(1)}, u32[]{:S(2)}, u32[]{:S(2)}) async-start(f32[8,1,1280]{2,1,0:T(1,128)} %broadcast_in_dim.59), calls=%async_computation | async-start | bytes 81920 | tf_op jit(solution)/shard_map/all_to_all | solution.py:33
  107.9 84.8 %reduce-scatter.2.cloned.1.call-start = ((), (), s32[]{:S(2)}) async-start(), calls=%async_computation.7 | async-start | bytes 11796480 | tf_op jit(solution)/shard_map/reduce_scatter | solution.py:110
  131.3 0.7 copy-start.2
  131.3 62.8 %copy-start.1 = (s32[160]{0:T(256)S(1)}, s32[160]{0:T(256)}, u32[]{:S(2)}) copy-start(s32[160]{0:T(256)} %param.10) | copy-start | bytes 1924
  137.7 15.8 %all-to-all-start.2 = ((f32[8,4,1,2048]{3,1,2,0:T(4,128)}), f32[8,4,1,2048]{3,1,2,0:T(4,128)S(1)}, u32[]{:S(2)}, u32[]{:S(2)}) async-start(f32[8,4,1,2048]{3,1,2,0:T(4,128)} %select_n.68), calls=%async_computation.3 | async-start | bytes 524288 | tf_op jit(solution)/shard_map/all_to_all | solution.py:88
  154.4 42.4 %all-to-all-start.3 = ((f32[8,4,1,2048]{3,0,2,1:T(8,128)}), f32[8,4,1,2048]{3,0,2,1:T(8,128)S(1)}, u32[]{:S(2)}, u32[]{:S(2)}) async-start(f32[8,4,1,2048]{3,0,2,1:T(8,128)} %copy.48), calls=%async_computation.4 | async-start | bytes 524288 | tf_op jit(solution)/shard_map/all_to_all | solution.py:88
  196.8 10.4 %copy-start = (f32[8,4,1,2048]{3,0,2,1:T(8,128)}, f32[8,4,1,2048]{3,0,2,1:T(8,128)S(1)}, u32[]{:S(2)}) copy-start(f32[8,4,1,2048]{3,0,2,1:T(8,128)S(1)} %all-to-all-done.3) | copy-start | bytes 786436
  196.8 18.8 %all-to-all-start.1 = ((f32[32,1,480]{2,1,0:T(1,128)}), f32[32,1,480]{2,1,0:T(1,128)S(1)}, u32[]{:S(2)}, u32[]{:S(2)}) async-start(f32[32,1,480]{2,1,0:T(1,128)} %reshape.248), calls=%async_computation.2 | async-start | bytes 131072 | tf_op jit(solution)/shard_map/all_to_all | solution.py:33
  222.2 13.8 %all-to-all-start.4 = ((f32[32,1,32]{2,1,0:T(1,128)}), f32[32,1,32]{2,1,0:T(1,128)S(1)}, u32[]{:S(2)}, u32[]{:S(2)}) async-start(f32[32,1,32]{2,1,0:T(1,128)} %broadcast_in_dim.72), calls=%async_computation.5 | async-start | bytes 32768 | tf_op jit(solution)/shard_map/all_to_all | solution.py:33
Sparse Core Ops, SparseCore 0:
  11.1 88.2 all-gather.1
  131.5 61.1 reduce-scatter.1
where the time goes:
time: 245 us
  waiting for transfers between devices  151 us (62%)
  starting transfers between devices  29 us (12%)
  matrix products  17.9 us (7%)
  other arithmetic  17.3 us (7%)
  between operations  16.2 us (7%)
  local copies, waits for them, and re-layouts  12.9 us (5%)
    all_gather x1, waiting for transfers between devices, gather_turned(): out = lax.all_gather(both, axis, axis=0, tiled=True)  89.8 us
    reduce_scatter x1, waiting for transfers between devices, shards(): lax.psum_scatter(jnp.dot(normed, head_weight, preferred_element_type=jnp....  33.1 us
    all_to_all x3, starting transfers between devices, sent_to_all(): lax.all_to_all(jnp.broadcast_to(shard[None], (devices, *shard.shape)), ax...  19.7 us
    dot_general x1, matrix products, shards(): jnp.dot(normed, head_weight, preferred_element_type=jnp.float32)  17.9 us
    all_to_all x3, waiting for transfers between devices, sent_to_all(): lax.all_to_all(jnp.broadcast_to(shard[None], (devices, *shard.shape)), ax...  16.7 us
    all_to_all x2, waiting for transfers between devices, exchange_in_order(): out = lax.all_to_all(out, axes[k], k, k, tiled=True)  11.8 us
    all_to_all x2, starting transfers between devices, exchange_in_order(): out = lax.all_to_all(out, axes[k], k, k, tiled=True)  9.18 us
  transfers between devices with their start and end apart: 7, of which 6 were waited for; matrix products, arithmetic and copies ran while one was open for 6% of the time, Pallas kernels for 0%

commit v1 on v0

v1 whole, which is shorter than its diff:
```python
import jax
import jax.numpy as jnp
from jax import lax
from jax.experimental import pallas as pl
from jax.experimental.pallas import tpu as pltpu
from jax.sharding import Mesh
from jax.sharding import PartitionSpec as P

D = 16384
VOCAB = 65536
POS = 5
EPS = 1e-05
NY, NC, NZ, NX = 4, 2, 8, 4
OWNERS = NY * NC
CHUNKS = 5
TOKENS = 1280
CT = TOKENS // CHUNKS
PIECE = CT // OWNERS
FEAT = 64
BLOCK = FEAT * NZ * NX
WIDTH = VOCAB // (NZ * NX)
HALF = WIDTH // 2
ROWS = TOKENS // OWNERS
KINDS = ("z", "x", "z", "x", "z")
MESH = pl.DeviceIdType.MESH
TENSOR = ("z", "x")
DP = ("y", "core")
F32 = jnp.float32
BF16 = jnp.bfloat16


def wrapped(i, n):
    return lax.rem(i + n, n)


def send(src, dst, send_sem, recv_sem, device):
    pltpu.make_async_remote_copy(
        src_ref=src, dst_ref=dst, send_sem=send_sem, recv_sem=recv_sem, device_id=device, device_id_type=MESH
    ).start()


def got(ref, sem):
    pltpu.make_async_copy(ref, ref, sem).wait()


def head_kernel(
    hid_hbm, gain_ref, w_hbm, out_ref,
    hid, g, w, xt, part, pair, r1p, r1m, r2p, r2m, gcol, rs,
    sx_out, sx_in, sz_in, sc_out, sc_in, sy_in,
    local_sem, g_send, g_recv, r_send, r_recv, s_send, s_recv,
):
    y, core = lax.axis_index("y"), lax.axis_index("core")
    z, x = lax.axis_index("z"), lax.axis_index("x")
    d = 1 - 2 * core
    zf, zb = wrapped(z + d, NZ), wrapped(z - d, NZ)
    xf, xb = wrapped(x + d, NX), wrapped(x - d, NX)
    yp, ym = wrapped(y + 1, NY), wrapped(y - 1, NY)
    other = 1 - core

    hid_in = pltpu.make_async_copy(hid_hbm, hid, local_sem.at[0])
    hid_in.start()
    w_in = pltpu.make_async_copy(w_hbm, w, local_sem.at[1])
    w_in.start()

    barrier = pltpu.get_barrier_semaphore()
    for k in range(1, NZ):
        pl.semaphore_signal(barrier, inc=1, device_id={"z": wrapped(z + k, NZ)}, device_id_type=MESH)
    for k in range(1, NX):
        pl.semaphore_signal(barrier, inc=1, device_id={"x": wrapped(x + k, NX)}, device_id_type=MESH)
    for k in range(1, NY):
        pl.semaphore_signal(barrier, inc=1, device_id={"y": wrapped(y + k, NY)}, device_id_type=MESH)
    pl.semaphore_signal(barrier, inc=1, device_id={"core": other}, device_id_type=MESH)

    def block(c, zz, xx):
        return g.at[c, pl.ds(pl.multiple_of((zz * NX + xx) * FEAT, FEAT), FEAT), :]

    def line(c, zz):
        return g.at[c, pl.ds(pl.multiple_of(zz * (NX * FEAT), NX * FEAT), NX * FEAT), :]

    def zat(k):
        return wrapped(z + d * k, NZ)

    hid_in.wait()
    lanes = lax.broadcasted_iota(jnp.int32, (FEAT, 128), 1) // PIECE
    mine = pl.ds(pl.multiple_of((z * NX + x) * FEAT, FEAT), FEAT)
    sx_out[...] = jnp.zeros_like(sx_out)
    for c in range(CHUNKS):
        for h in range(2):
            tile = jnp.zeros((FEAT, 128), F32)
            for j in range(4):
                place = h * 4 + j
                owner = (place % NY) * NC + place // NY
                start = owner * ROWS + PIECE * c
                at, off = start // 128, start % 128
                source = hid[:, at * 128 : at * 128 + 128].astype(F32)
                shift = (PIECE * j - off) % 128
                moved = pltpu.roll(source, shift, 1) if shift else source
                tile = jnp.where(lanes == j, moved, tile)
            g[c, mine, h * 128 : h * 128 + 128] = tile.astype(BF16)
            sx_out[2 * c + h : 2 * c + h + 1, :] = jnp.sum(tile * tile, axis=0, keepdims=True)
    both = jnp.concatenate([gain_ref[...].astype(F32)] * 2, axis=1)
    lane = lax.broadcasted_iota(jnp.int32, (1, 128), 1) // FEAT
    sx_out[10:11, :] = jnp.where(lane == lax.rem(x, 2), both, 0.0)

    pl.semaphore_wait(barrier, NZ + NX + NY - 3 + 1)

    def z_first(c):
        def pass_on(k, zz, device):
            ref = block(c, zz, x)
            send(ref, ref, g_send.at[c], g_recv.at[c, k], {"z": device})

        def arrived(k, zz):
            got(block(c, zz, x), g_recv.at[c, k])

        def across(ks, xx, device, k):
            for kk in ks:
                ref = block(c, zat(kk), xx)
                send(ref, ref, g_send.at[c], g_recv.at[c, k], {"x": device})

        def group(count, k):
            got(g.at[c, pl.ds(0, count * FEAT), :], g_recv.at[c, k])

        near, far = (0, -1, 1, -2, 2), (-3, 3, -4)

        def s0():
            pass_on(0, z, zf)
            pass_on(4, z, zb)

        def s1():
            arrived(0, zat(-1))
            pass_on(1, zat(-1), zf)
            arrived(4, zat(1))
            pass_on(5, zat(1), zb)

        def s2():
            arrived(1, zat(-2))
            pass_on(2, zat(-2), zf)
            arrived(5, zat(2))
            pass_on(6, zat(2), zb)
            across(near, x, xf, 7)
            across(near, x, xb, 8)

        def s3():
            arrived(2, zat(-3))
            pass_on(3, zat(-3), zf)
            arrived(6, zat(3))

        def s4():
            arrived(3, zat(-4))
            across(far, x, xf, 9)
            across(far, x, xb, 10)
            group(5, 7)
            across(near, xb, xf, 11)
            group(5, 8)

        def s5():
            group(3, 9)
            group(3, 10)
            across(far, xf, xb, 12)

        def s6():
            group(5, 11)
            group(3, 12)

        return [s0, s1, s2, s3, s4, s5, s6]

    def x_first(c):
        def pass_on(k, zz, device):
            ref = line(c, zz)
            send(ref, ref, g_send.at[c], g_recv.at[c, k], {"z": device})

        def arrived(k, zz):
            got(line(c, zz), g_recv.at[c, k])

        def s0():
            for k in range(1, NX):
                ref = block(c, z, x)
                send(ref, ref, g_send.at[c], g_recv.at[c, 6 + k], {"x": wrapped(x + k, NX)})

        def s1():
            for k in range(1, NX):
                got(block(c, z, wrapped(x - k, NX)), g_recv.at[c, 6 + k])
            pass_on(0, z, zf)
            pass_on(4, z, zb)

        def s2():
            arrived(0, zat(-1))
            pass_on(1, zat(-1), zf)
            arrived(4, zat(1))
            pass_on(5, zat(1), zb)

        def s3():
            arrived(1, zat(-2))
            pass_on(2, zat(-2), zf)
            arrived(5, zat(2))
            pass_on(6, zat(2), zb)

        def s4():
            arrived(2, zat(-3))
            pass_on(3, zat(-3), zf)
            arrived(6, zat(3))

        def s5():
            arrived(3, zat(-4))

        return [s0, s1, s2, s3, s4, s5]

    def q0():
        for k in range(1, NX):
            send(sx_out, sx_in.at[k - 1], s_send.at[0], s_recv.at[k - 1], {"x": wrapped(x + k, NX)})

    def q1():
        for k in range(1, NX):
            got(sx_in.at[k - 1], s_recv.at[k - 1])
        total = sx_out[0:10, :] + sx_in[0, 0:10, :] + sx_in[1, 0:10, :] + sx_in[2, 0:10, :]
        sz_in[z, 0:10, :] = total
        own = sx_out[10:11, :]
        one, two, three = sx_in[0, 10:11, :], sx_in[1, 10:11, :], sx_in[2, 10:11, :]
        odd = lax.rem(x, 2) == 1
        with_next = jnp.where(odd, one, three)
        first = jnp.where(odd, three, one)
        mate = own + with_next
        rest = two + first
        low = x < 2
        sz_in[z, 10:11, :] = jnp.where(low, mate, rest)
        sz_in[z, 11:12, :] = jnp.where(low, rest, mate)
        for k in range(1, NZ):
            send(sz_in.at[z], sz_in.at[z], s_send.at[1], s_recv.at[2 + k], {"z": wrapped(z + k, NZ)})

    def q2():
        for k in range(1, NZ):
            got(sz_in.at[wrapped(z - k, NZ)], s_recv.at[2 + k])
        total = sz_in[0, 0:10, :]
        for k in range(1, NZ):
            total = total + sz_in[k, 0:10, :]
        sc_out[0:10, :] = total
        send(sc_out, sc_in, s_send.at[2], s_recv.at[10], {"core": other})
        for k in range(NZ):
            for half in range(2):
                row = jnp.broadcast_to(sz_in[k, 10 + half : 11 + half, :], (128, 128))
                gcol[pl.ds((2 * k + half) * 128, 128), :] = row.T

    def q3():
        got(sc_in, s_recv.at[10])
        sy_in[y, 0:10, :] = sc_out[0:10, :] + sc_in[0:10, :]
        for k in range(1, NY):
            send(sy_in.at[y], sy_in.at[y], s_send.at[3], s_recv.at[10 + k], {"y": wrapped(y + k, NY)})

    def q4():
        for k in range(1, NY):
            got(sy_in.at[wrapped(y - k, NY)], s_recv.at[10 + k])
        total = (sy_in[0, 0:10, :] + sy_in[1, 0:10, :]) + (sy_in[2, 0:10, :] + sy_in[3, 0:10, :])
        rs[0:10, :] = lax.rsqrt(total / D + EPS)

    def compute(c):
        scale = [jnp.broadcast_to(rs[2 * c + h : 2 * c + h + 1, :], (128, 128)) for h in range(2)]

        @pl.loop(0, BLOCK // 128)
        def _(k):
            rows = pl.ds(pl.multiple_of(k * 128, 128), 128)
            gains = gcol[rows, :]
            for h in range(2):
                values = g[c, rows, h * 128 : h * 128 + 128].astype(F32)
                normed = (values * scale[h] * gains).astype(BF16)
                xt[h * 128 : h * 128 + 128, rows] = normed.T

        if c == 0:
            w_in.wait()

        @pl.loop(0, WIDTH // 256)
        def _(k):
            columns = pl.ds(pl.multiple_of(k * 256, 256), 256)
            part[c, :, columns] = jnp.dot(xt[...], w[:, columns], preferred_element_type=F32)

        theirs = pl.ds(pl.multiple_of(other * 128, 128), 128)
        send(part.at[c, theirs, :], pair.at[c], r_send.at[c], r_recv.at[c, 0], {"core": other})

    def own_rows(yy):
        return pl.ds(pl.multiple_of(core * 128 + yy * PIECE, PIECE), PIECE)

    low, high = pl.ds(0, HALF), pl.ds(HALF, HALF)

    def reduce_a(c):
        got(pair.at[c], r_recv.at[c, 0])

        def add(yy):
            rows = own_rows(yy)
            part[c, rows, :] = part[c, rows, :] + pair[c, pl.ds(pl.multiple_of(yy * PIECE, PIECE), PIECE), :]

        across = wrapped(y + 2, NY)
        add(across)
        send(part.at[c, own_rows(across), low], r1p.at[c], r_send.at[c], r_recv.at[c, 1], {"y": yp})
        send(part.at[c, own_rows(across), high], r1m.at[c], r_send.at[c], r_recv.at[c, 2], {"y": ym})
        add(yp)
        send(part.at[c, own_rows(yp), high], r2p.at[c, :, high], r_send.at[c], r_recv.at[c, 3], {"y": yp})
        add(ym)
        send(part.at[c, own_rows(ym), low], r2m.at[c, :, low], r_send.at[c], r_recv.at[c, 4], {"y": ym})
        add(y)

    def reduce_b(c):
        got(r1p.at[c], r_recv.at[c, 1])
        rows = own_rows(yp)
        part[c, rows, 0:HALF] = part[c, rows, 0:HALF] + r1p[c]
        send(part.at[c, rows, low], r2p.at[c, :, low], r_send.at[c], r_recv.at[c, 5], {"y": yp})
        got(r1m.at[c], r_recv.at[c, 2])
        rows = own_rows(ym)
        part[c, rows, HALF:WIDTH] = part[c, rows, HALF:WIDTH] + r1m[c]
        send(part.at[c, rows, high], r2m.at[c, :, high], r_send.at[c], r_recv.at[c, 6], {"y": ym})

    def reduce_c(c):
        got(r2p.at[c, :, high], r_recv.at[c, 3])
        got(r2m.at[c, :, low], r_recv.at[c, 4])
        got(r2p.at[c, :, low], r_recv.at[c, 5])
        got(r2m.at[c, :, high], r_recv.at[c, 6])
        out_ref[c * PIECE : (c + 1) * PIECE, :] = part[c, own_rows(y), :] + (r2p[c] + r2m[c])

    steps = {"z": z_first, "x": x_first}
    gather = [steps[kind](c) for c, kind in enumerate(KINDS)]
    squares = [q0, q1, q2, q3, q4]
    done = 0
    pending_a, pending_b = [], []
    rounds = max(2 * c + len(gather[c]) for c in range(CHUNKS))
    for r in range(rounds):
        for c in range(CHUNKS):
            if 0 <= r - 2 * c < len(gather[c]):
                gather[c][r - 2 * c]()
        if r < len(squares):
            squares[r]()
        while pending_b and pending_b[0][1] <= r:
            reduce_b(pending_b.pop(0)[0])
        while pending_a and pending_a[0][1] <= r:
            c = pending_a.pop(0)[0]
            reduce_a(c)
            pending_b.append((c, r + 2))
        while done < CHUNKS and 2 * done + len(gather[done]) - 1 <= r:
            compute(done)
            pending_a.append((done, r + 1))
            done += 1
    for c, _ in list(pending_b):
        reduce_b(c)
    pending_b = []
    for c, _ in pending_a:
        reduce_a(c)
        pending_b.append((c, 0))
    for c, _ in pending_b:
        reduce_b(c)
    for c in range(CHUNKS):
        reduce_c(c)

    for c in range(CHUNKS):
        got(g.at[c, pl.ds(0, 31 * FEAT), :], g_send.at[c])
        got(part.at[c, pl.ds(0, 224), :], r_send.at[c])
    got(sx_in, s_send.at[0])
    got(sz_in.at[pl.ds(0, NZ - 1)], s_send.at[1])
    got(sc_in, s_send.at[2])
    got(sy_in.at[pl.ds(0, NY - 1)], s_send.at[3])


def owned_logits(hidden, gain, head_weight):
    vmem = pltpu.VMEM
    dma = pltpu.SemaphoreType.DMA
    return pl.pallas_call(
        head_kernel,
        out_shape=jax.ShapeDtypeStruct((ROWS, WIDTH), F32),
        in_specs=[
            pl.BlockSpec(memory_space=pl.ANY),
            pl.BlockSpec(memory_space=pltpu.VMEM),
            pl.BlockSpec(memory_space=pl.ANY),
        ],
        out_specs=pl.BlockSpec(memory_space=pltpu.VMEM),
        scratch_shapes=[
            vmem((FEAT, TOKENS), BF16),
            vmem((CHUNKS, BLOCK, CT), BF16),
            vmem((BLOCK, WIDTH), BF16),
            vmem((CT, BLOCK), BF16),
            vmem((CHUNKS, CT, WIDTH), F32),
            vmem((CHUNKS, CT // 2, WIDTH), F32),
            vmem((CHUNKS, PIECE, HALF), F32),
            vmem((CHUNKS, PIECE, HALF), F32),
            vmem((CHUNKS, PIECE, WIDTH), F32),
            vmem((CHUNKS, PIECE, WIDTH), F32),
            vmem((BLOCK, 128), F32),
            vmem((16, 128), F32),
            vmem((16, 128), F32),
            vmem((NX - 1, 16, 128), F32),
            vmem((NZ, 16, 128), F32),
            vmem((16, 128), F32),
            vmem((16, 128), F32),
            vmem((NY, 16, 128), F32),
            dma((2,)),
            dma((CHUNKS,)),
            dma((CHUNKS, 13)),
            dma((CHUNKS,)),
            dma((CHUNKS, 7)),
            dma((4,)),
            dma((14,)),
        ],
        compiler_params=pltpu.CompilerParams(
            collective_id=0, has_side_effects=True, vmem_limit_bytes=60 * 1024 * 1024
        ),
        name="head",
    )(hidden.T, gain, head_weight)


def sent_to_all(shard, axis):
    devices = lax.axis_size(axis)
    return lax.all_to_all(
        jnp.broadcast_to(shard[None], (devices, *shard.shape)), axis, 0, 0, tiled=True
    )


def exchanged(local_rows):
    out = local_rows.reshape(NZ, NX, 1, WIDTH)
    out = lax.all_to_all(out, "z", 0, 0, tiled=True)
    out = lax.all_to_all(out, "x", 1, 1, tiled=True)
    return out.reshape(NZ * NX, WIDTH)


def shards(hidden, gain, head_weight, draft_probs, draft_ids, reject_at):
    owned = draft_probs.shape[0] // POS
    mine = lax.dynamic_slice_in_dim(reject_at, lax.axis_index(TENSOR) * owned, owned, 0)
    local_rows = jnp.take_along_axis(
        draft_probs.reshape(owned, POS, draft_probs.shape[1]), mine[:, None, None], axis=1
    )[:, 0]
    drafts = exchanged(local_rows)
    logits = owned_logits(hidden, gain, head_weight)
    width = logits.shape[1]
    columns = lax.broadcasted_iota(jnp.int32, (1, width), 1) + lax.axis_index(TENSOR) * width
    local_max = jnp.max(logits, axis=1)
    local_pick = jnp.sum(jnp.where(columns == draft_ids[:, None], logits, 0.0), axis=1)
    local_total = jnp.sum(jnp.exp(logits - local_max[:, None]), axis=1)
    stats = sent_to_all(jnp.stack([local_max, local_total, local_pick]), TENSOR)
    tops, totals, picks = stats[:, 0], stats[:, 1], stats[:, 2]
    top = jnp.max(tops, axis=0)
    total = jnp.sum(totals * jnp.exp(tops - top), axis=0)
    picked = jnp.sum(picks, axis=0)
    logz = top + jnp.log(total)
    token_logprob = picked - logz
    requests = reject_at.shape[0]
    hot = lax.broadcasted_iota(jnp.int32, (requests, POS), 1) == reject_at[:, None]
    chosen = jnp.sum(jnp.where(hot[:, :, None], logits.reshape(requests, POS, width), 0.0), axis=1)
    chosen_logz = jnp.sum(jnp.where(hot, logz.reshape(requests, POS), 0.0), axis=1)
    target = jnp.exp(chosen - chosen_logz[:, None])
    kept = jnp.maximum(target - drafts, 0.0)
    mass = jnp.sum(sent_to_all(jnp.sum(kept, axis=1), TENSOR), axis=0)
    residual = VOCAB * kept / mass[:, None]
    return (token_logprob, residual)


def solution(mesh):
    finer = Mesh(mesh.devices.reshape(NY, NC, NZ, NX), ("y", "core", "z", "x"))
    return jax.shard_map(
        shards,
        mesh=finer,
        in_specs=(
            P(None, (*DP, *TENSOR)),
            P(None, (*DP, *TENSOR)),
            P(DP, TENSOR),
            P((*DP, *TENSOR), None),
            P(DP),
            P(DP),
        ),
        out_specs=(P(DP), P(DP, TENSOR)),
        check_vma=False,
    )
```

time: 245 us -> 164 us (0.67)
  waiting for transfers between devices: 151 us -> 23.9 us
  Pallas kernels: 0 us -> 101 us
  matrix products: 17.9 us -> 0 us
  between operations: 16.2 us -> 2.73 us
  other arithmetic: 17.3 us -> 8.17 us
  starting transfers between devices: 29 us -> 21.6 us
  local copies, waits for them, and re-layouts: 12.9 us -> 5.54 us
    pallas_call x0 -> x1, Pallas kernels: none -> 101 us  [owned_logits(): pl.pallas_call(head_kernel, out_shape=jax.ShapeDtypeStruct((ROWS, WIDTH),...]
    all_gather x1 -> x0, waiting for transfers between devices: 89.8 us -> none  [gather_turned(): out = lax.all_gather(both, axis, axis=0, tiled=True)]
    reduce_scatter x1 -> x0, waiting for transfers between devices: 33.1 us -> none  [shards(): lax.psum_scatter(jnp.dot(normed, head_weight, preferred_element_type=jnp....]
    dot_general x1 -> x0, matrix products: 17.9 us -> none  [shards(): jnp.dot(normed, head_weight, preferred_element_type=jnp.float32)]
    all_to_all x3 -> x2, starting transfers between devices: 19.7 us -> 12.4 us  [sent_to_all(): lax.all_to_all(jnp.broadcast_to(shard[None], (devices, *shard.shape)), ax...]
    all_to_all x3 -> x2, waiting for transfers between devices: 16.7 us -> 10.7 us  [sent_to_all(): lax.all_to_all(jnp.broadcast_to(shard[None], (devices, *shard.shape)), ax...]
    reduce_sum x4 -> x5, other arithmetic: 4.88 us -> 1.35 us  [the longest x1 0.79 us: shards(): jnp.sum(jnp.where(hot[:, :, None], logits.reshape(requests, POS, width),...]
  transfers between devices with their start and end apart: 7 -> 4, of which waited for: 6 -> 4; matrix products, arithmetic and copies ran while one was open for 6% -> 5% of each run, Pallas kernels for 0% -> 0%
where the time goes in v1:
time: 164 us; the launch traced here: 163 us
  Pallas kernels  101 us (62%)
  waiting for transfers between devices  23.9 us (15%)
  starting transfers between devices  21.6 us (13%)
  other arithmetic  8.17 us (5%)
  local copies, waits for them, and re-layouts  5.54 us (3%)
  between operations  2.73 us (2%)
    pallas_call x1, Pallas kernels, owned_logits(): pl.pallas_call(head_kernel, out_shape=jax.ShapeDtypeStruct((ROWS, WIDTH),...  101 us
    all_to_all x2, starting transfers between devices, sent_to_all(): lax.all_to_all(jnp.broadcast_to(shard[None], (devices, *shard.shape)), ax...  12.4 us
    all_to_all x2, waiting for transfers between devices, sent_to_all(): lax.all_to_all(jnp.broadcast_to(shard[None], (devices, *shard.shape)), ax...  10.7 us
    all_to_all x1, waiting for transfers between devices, exchanged(): out = lax.all_to_all(out, 'z', 0, 0, tiled=True)  8.86 us
    all_to_all x1, starting transfers between devices, exchanged(): out = lax.all_to_all(out, 'x', 1, 1, tiled=True)  4.8 us
    all_to_all x1, starting transfers between devices, exchanged(): out = lax.all_to_all(out, 'z', 0, 0, tiled=True)  4.44 us
    all_to_all x1, waiting for transfers between devices, exchanged(): out = lax.all_to_all(out, 'x', 1, 1, tiled=True)  4.29 us
  transfers between devices with their start and end apart: 4, of which 4 were waited for; matrix products, arithmetic and copies ran while one was open for 5% of the time, Pallas kernels for 0%

profile of v1, /device:TPU:2, one launch (start us, length us, event | category | flops | bytes accessed | tf_op | source)
XLA Modules:
  0.0 163.2 jit_solution(1287258304265002287)
XLA Ops:
  0.6 101.3 %head.1 = f32[160,2048]{1,0:T(8,128)} custom-call(bf16[64,1280]{1,0:T(8,128)(2,1)} %bitcast.22, bf16[1,64]{1,0:T(2,128)(2,1)} %gain_ref.1, bf16[2048,2048]{1,0:T(8,128)(2,1)} %w_hbm.1), custom_call_target="tpu_custom_call" | custom-call | tf_op jit(solution)/shard_map/head/pallas_call | solution.py:362
  102.0 0.0 copy-start
  102.0 0.0 copy-start.2
  102.0 1.6 reduce_max.18
  103.5 0.1 copy-done
  103.7 0.0 copy-done.2
  103.7 0.4 exponential_reduce_fusion
  104.2 0.8 reshape.144
  105.0 7.5 %all-to-all-start = ((f32[32,1,480]{2,1,0:T(1,128)}), f32[32,1,480]{2,1,0:T(1,128)S(1)}, u32[]{:S(2)}, u32[]{:S(2)}) async-start(f32[32,1,480]{2,1,0:T(1,128)} %reshape.144), calls=%async_computation | async-start | bytes 131072 | tf_op jit(solution)/shard_map/all_to_all | solution.py:407
  112.5 0.0 copy-start.1
  112.5 0.2 reshape.99
  112.7 0.4 copy-done.1
  113.1 0.6 dynamic_slice.3
  115.7 2.4 %fusion = f32[65536]{0:T(1024)S(1)} fusion(pred[]{:T(512)} %bitcast.6, f32[5,65536]{1,0:T(8,128)} %param.9, s32[]{:T(128)} %bitcast.7), kind=kLoop, calls=%fused_computation.4 | loop fusion | flops 65536 | bytes 524293 | tf_op jit(solution)/shard_map/jit(take_along_axis)/select_n | solution.py:422
  118.1 0.8 select_n.41
  118.9 0.1 iota_compare_fusion
  118.9 2.2 %all-to-all-done = f32[32,1,480]{2,1,0:T(1,128)S(1)} async-done(((f32[32,1,480]{2,1,0:T(1,128)}), f32[32,1,480]{2,1,0:T(1,128)S(1)}, u32[]{:S(2)}, u32[]{:S(2)}) %all-to-all-start) | async-done | bytes 61472 | tf_op jit(solution)/shard_map/all_to_all | solution.py:407
  121.2 4.4 %all-to-all-start.1 = ((f32[8,4,1,2048]{3,1,2,0:T(4,128)}), f32[8,4,1,2048]{3,1,2,0:T(4,128)S(1)}, u32[]{:S(2)}, u32[]{:S(2)}) async-start(f32[8,4,1,2048]{3,1,2,0:T(4,128)} %select_n.41), calls=%async_computation.1 | async-start | bytes 524288 | tf_op jit(solution)/shard_map/all_to_all | solution.py:414
  125.6 0.8 select_reduce_fusion
  126.4 0.1 reduce_sum.80
  126.5 0.5 broadcast.85
  127.0 0.8 reduce.8
  127.8 0.1 reshape.145
  127.9 0.1 fusion.6
  128.1 8.9 %all-to-all-done.1 = f32[8,4,1,2048]{3,1,2,0:T(4,128)S(1)} async-done(((f32[8,4,1,2048]{3,1,2,0:T(4,128)}), f32[8,4,1,2048]{3,1,2,0:T(4,128)S(1)}, u32[]{:S(2)}, u32[]{:S(2)}) %all-to-all-start.1) | async-done | bytes 262176 | tf_op jit(solution)/shard_map/all_to_all | solution.py:414
  136.9 0.9 copy.22
  137.8 4.8 %all-to-all-start.2 = ((f32[8,4,1,2048]{3,0,2,1:T(8,128)}), f32[8,4,1,2048]{3,0,2,1:T(8,128)S(1)}, u32[]{:S(2)}, u32[]{:S(2)}) async-start(f32[8,4,1,2048]{3,0,2,1:T(8,128)} %copy.22), calls=%async_computation.2 | async-start | bytes 524288 | tf_op jit(solution)/shard_map/all_to_all | solution.py:415
  142.6 0.6 fusion.5
  143.2 0.1 add.33
  143.3 0.2 select_reduce_fusion.2
  143.4 0.1 sub.54
  143.5 4.3 %all-to-all-done.2 = f32[8,4,1,2048]{3,0,2,1:T(8,128)S(1)} async-done(((f32[8,4,1,2048]{3,0,2,1:T(8,128)}), f32[8,4,1,2048]{3,0,2,1:T(8,128)S(1)}, u32[]{:S(2)}, u32[]{:S(2)}) %all-to-all-start.2) | async-done | bytes 262176 | tf_op jit(solution)/shard_map/all_to_all | solution.py:415
  147.8 0.3 maximum_reduce_fusion
  148.1 0.1 broadcast_in_dim.60
  148.2 0.6 broadcast_in_dim.61
  148.8 4.9 %all-to-all-start.3 = ((f32[32,1,32]{2,1,0:T(1,128)}), f32[32,1,32]{2,1,0:T(1,128)S(1)}, u32[]{:S(2)}, u32[]{:S(2)}) async-start(f32[32,1,32]{2,1,0:T(1,128)} %broadcast_in_dim.61), calls=%async_computation.3 | async-start | bytes 32768 | tf_op jit(solution)/shard_map/all_to_all | solution.py:407
  153.8 0.1 reshape.102
  153.9 8.5 %all-to-all-done.3 = f32[32,1,32]{2,1,0:T(1,128)S(1)} async-done(((f32[32,1,32]{2,1,0:T(1,128)}), f32[32,1,32]{2,1,0:T(1,128)S(1)}, u32[]{:S(2)}, u32[]{:S(2)}) %all-to-all-start.3) | async-done | bytes 4128 | tf_op jit(solution)/shard_map/all_to_all | solution.py:407
  162.4 0.8 multiply_divide_fusion
  (5 shorter events, 0.1 us)
Async XLA Ops:
  102.0 1.7 %copy-start = (f32[160,2048]{1,0:T(8,128)S(1)}, f32[160,2048]{1,0:T(8,128)}, u32[]{:S(2)}) copy-start(f32[160,2048]{1,0:T(8,128)} %head.1) | copy-start | bytes 3932164
  102.0 1.7 %copy-start.2 = (s32[160]{0:T(256)S(1)}, s32[160]{0:T(256)}, u32[]{:S(2)}) copy-start(s32[160]{0:T(256)} %param.10) | copy-start | bytes 1924
  105.0 16.2 %all-to-all-start = ((f32[32,1,480]{2,1,0:T(1,128)}), f32[32,1,480]{2,1,0:T(1,128)S(1)}, u32[]{:S(2)}, u32[]{:S(2)}) async-start(f32[32,1,480]{2,1,0:T(1,128)} %reshape.144), calls=%async_computation | async-start | bytes 131072 | tf_op jit(solution)/shard_map/all_to_all | solution.py:407
  112.5 0.7 copy-start.1
  121.2 15.8 %all-to-all-start.1 = ((f32[8,4,1,2048]{3,1,2,0:T(4,128)}), f32[8,4,1,2048]{3,1,2,0:T(4,128)S(1)}, u32[]{:S(2)}, u32[]{:S(2)}) async-start(f32[8,4,1,2048]{3,1,2,0:T(4,128)} %select_n.41), calls=%async_computation.1 | async-start | bytes 524288 | tf_op jit(solution)/shard_map/all_to_all | solution.py:414
  137.8 10.0 %all-to-all-start.2 = ((f32[8,4,1,2048]{3,0,2,1:T(8,128)}), f32[8,4,1,2048]{3,0,2,1:T(8,128)S(1)}, u32[]{:S(2)}, u32[]{:S(2)}) async-start(f32[8,4,1,2048]{3,0,2,1:T(8,128)} %copy.22), calls=%async_computation.2 | async-start | bytes 524288 | tf_op jit(solution)/shard_map/all_to_all | solution.py:415
  148.8 13.5 %all-to-all-start.3 = ((f32[32,1,32]{2,1,0:T(1,128)}), f32[32,1,32]{2,1,0:T(1,128)S(1)}, u32[]{:S(2)}, u32[]{:S(2)}) async-start(f32[32,1,32]{2,1,0:T(1,128)} %broadcast_in_dim.61), calls=%async_computation.3 | async-start | bytes 32768 | tf_op jit(solution)/shard_map/all_to_all | solution.py:407
